TPU v7x, 32 devices: a whole 2x2x4 slice. The times are simulated.
32 devices in a mesh: gx: 8 (over z, x), gy: 4 (over y, core).
Axes of the slice: x: 2, y: 2, z: 4, core: 2. Of those that a mesh axis runs over, the one named last changes fastest.
Arguments:
- velocity: float32 [3, 64, 256, 256], P(None, 'gx', 'gy'), may hold values from -10 to 10
Outputs:
- coefficient: float32 [256], P('gy')
- viscosity: float32 [64, 256, 256], P('gx', 'gy')
All inputs are finite; a program needn't handle non-finite values.
Results may differ from a plain program's by a relative error of at most 0.00002.
Values sent between devices are 32-bit elements; how exact they have to be, the bound alone decides.
A program may use at most 64 MiB of HBM per device.

v0:
```python
import functools

import jax
import jax.numpy as jnp
from jax import lax
from jax.experimental import pallas as pl
from jax.experimental.pallas import tpu as pltpu
from jax.sharding import PartitionSpec as P

clip_high = 0.1
pairs = ((0, 0), (1, 1), (2, 2), (0, 1), (0, 2), (1, 2))
MESH = pl.DeviceIdType.MESH
EARLY = 4


def tile(index):
    return pl.ds(pl.multiple_of(index * 8, 8), 8)


def roll_next(value):
    return pltpu.roll(value, value.shape[1] - 1, 1)


def roll_prev(value):
    return pltpu.roll(value, 1, 1)


def filter_span(value):
    return (roll_next(value) + roll_prev(value)) + 2.0 * value


def slope_span(value):
    return roll_next(value) - roll_prev(value)


def slope_wall(ref, comp, row, t, here):
    rows = lax.broadcasted_iota(jnp.int32, here.shape, 0)
    below = ref[comp, row, tile(t - 1), :]
    above = ref[comp, row, tile(t + 1), :]
    up = pltpu.roll(jnp.where(rows == 0, above, here), 7, 0)
    down = pltpu.roll(jnp.where(rows == 7, below, here), 1, 0)
    return up - down


def strain4(ref, row, t, slope=None):
    here = [ref[c, row, tile(t), :] for c in range(3)]
    dx = [ref[c, row + 1, tile(t), :] - ref[c, row - 1, tile(t), :] for c in range(3)]
    dy = [slope_wall(ref, c, row, t, here[c]) for c in range(3)]
    if slope is None:
        dz = [slope_span(here[c]) for c in range(3)]
    else:
        dz = [slope[c, row, tile(t), :] for c in range(3)]
    s = (
        dx[0],
        4.0 * dy[1],
        2.0 * dz[2],
        2.0 * dy[0] + 0.5 * dx[1],
        dz[0] + 0.5 * dx[2],
        dz[1] + 2.0 * dy[2],
    )
    diag = s[0] * s[0] + s[1] * s[1] + s[2] * s[2]
    off = s[3] * s[3] + s[4] * s[4] + s[5] * s[5]
    return here, s, diag + 2.0 * off


def kernel(n, m, nx, ny, u_hbm, strength, coef_ref, u, w, v, d, g, accn, accd,
           edge_out, edge_in, mine, mine_ends, gather, own_sem, xs_send, xs_recv, ys_send, ys_recv,
           c_send, c_recv, g_send, g_recv, ring):
    nt = ny // 8
    gx = lax.axis_index("gx")
    gy = lax.axis_index("gy")
    left, right = lax.rem(gx + n - 1, n), lax.rem(gx + 1, n)
    not_low, not_high = gy > 0, gy < m - 1
    lanes = mine.shape[-1]

    own = pltpu.make_async_copy(u_hbm, u.at[:, 2:2 + nx, 8:8 + ny, :], own_sem)
    own.start()

    barrier = pltpu.get_barrier_semaphore()

    def to_ends(semaphore):
        @pl.when(not_low)
        def _():
            pl.semaphore_signal(semaphore, inc=1, device_id=(gx, gy - 1), device_id_type=MESH)

        @pl.when(not_high)
        def _():
            pl.semaphore_signal(semaphore, inc=1, device_id=(gx, gy + 1), device_id_type=MESH)

    def to_sides(semaphore):
        for side in (left, right):
            pl.semaphore_signal(semaphore, inc=1, device_id=(side, gy), device_id_type=MESH)

    to_sides(barrier)
    to_ends(barrier)
    ends = jnp.where(not_low, 1, 0) + jnp.where(not_high, 1, 0)
    pl.semaphore_wait(barrier, ends + 2)
    own.wait()

    rounds = n // 2 - 1

    def open_round(k):
        if k < rounds:
            to_sides(ring.at[k])

    def close_round(k):
        if k < rounds:
            pl.semaphore_wait(ring.at[k], 2)

    def x_copy(side, t):
        src = 2 if side == 0 else nx
        dst = nx + 2 if side == 0 else 0
        return pltpu.make_async_remote_copy(
            src_ref=u.at[:, src:src + 2, tile(t), :],
            dst_ref=u.at[:, dst:dst + 2, tile(t), :],
            send_sem=xs_send.at[side],
            recv_sem=xs_recv.at[side, t - 1],
            device_id=(left if side == 0 else right, gy),
            device_id_type=MESH,
        )

    def x_all(side):
        part = u.at[:, 2:4, 8:8 + ny, :]
        return pltpu.make_async_remote_copy(
            src_ref=part,
            dst_ref=part,
            send_sem=xs_send.at[side],
            recv_sem=xs_recv.at[side, 0],
            device_id=(right, gy),
            device_id_type=MESH,
        )

    def y_copy(side):
        src = 8 if side == 0 else ny
        dst = ny + 8 if side == 0 else 0
        return pltpu.make_async_remote_copy(
            src_ref=u.at[:, 2:2 + nx, src:src + 8, :],
            dst_ref=u.at[:, 2:2 + nx, dst:dst + 8, :],
            send_sem=ys_send.at[side],
            recv_sem=ys_recv.at[side],
            device_id=(gx, gy - 1 if side == 0 else gy + 1),
            device_id_type=MESH,
        )

    def c_copy(side):
        return pltpu.make_async_remote_copy(
            src_ref=edge_out.at[side],
            dst_ref=edge_in.at[side],
            send_sem=c_send.at[side],
            recv_sem=c_recv.at[side],
            device_id=(left if side == 0 else right, gy),
            device_id_type=MESH,
        )

    @pl.when(not_low)
    def _():
        y_copy(0).start()

    @pl.when(not_high)
    def _():
        y_copy(1).start()

    def start_x(i, carry):
        t = jnp.where(i < 2, nt - i, i - 1)
        x_copy(0, t).start()
        x_copy(1, t).start()
        return carry

    lax.fori_loop(0, EARLY, start_x, 0)

    accn[...] = jnp.zeros_like(accn)
    accd[...] = jnp.zeros_like(accd)

    @pl.when(jnp.logical_not(not_low))
    def _():
        u[:, 2:2 + nx, 0:8, :] = jnp.zeros((3, nx, 8, u.shape[3]), jnp.float32)

    @pl.when(jnp.logical_not(not_high))
    def _():
        u[:, 2:2 + nx, ny + 8:ny + 16, :] = jnp.zeros((3, nx, 8, u.shape[3]), jnp.float32)

    @pl.when(not_high)
    def _():
        y_copy(0).wait_recv()

    @pl.when(not_low)
    def _():
        y_copy(1).wait_recv()

    for side in range(2):
        src = 2 if side == 0 else nx
        for c in range(3):
            for r in range(2):
                k = 2 * c + r
                edge_out[side, k:k + 1, :] = u[c, src + r, 7:8, :]
                edge_out[side, 6 + k:7 + k, :] = u[c, src + r, ny + 8:ny + 9, :]
    for side in range(2):
        c_copy(side).start()
    lax.fori_loop(EARLY, nt, start_x, 0)

    def span_rows(t, rows, slopes=True):
        for c in range(3):
            for row in rows:
                here = u[c, row, tile(t), :]
                after, before = roll_next(here), roll_prev(here)
                w[c, row, tile(t), :] = (after + before) + 2.0 * here
                if slopes:
                    d[c, row, tile(t), :] = after - before

    def filtered_rows(t, rows):
        for c in range(3):
            for row in rows:
                a, b, e = (w[c, row + k, tile(t), :] for k in (-1, 0, 1))
                v[c, row, tile(t), :] = 0.25 * ((a + e) + 2.0 * b)

    def stress_row(t, row, keep):
        _, s, total = strain4(u, row, t, d)
        size = jnp.sqrt(0.125 * total)
        if keep:
            strength[row - 2, tile(t - 1), :] = size
        for k in range(6):
            g[k, row, tile(t - 1), :] = size * s[k]

    def sums_row(t, row):
        centre, s, total = strain4(v, row, t)
        scale = jnp.sqrt(2.0 * total)

        def product(a, b):
            one, two, three = (near[j][a] * near[j][b] for j in range(3))
            return filter_span((one + three) + 2.0 * two)

        def stress(k):
            one, two, three = (g[k, row + j, tile(t - 1), :] for j in (-1, 0, 1))
            return filter_span((one + three) + 2.0 * two)

        near = [[u[c, row + j, tile(t), :] for c in range(3)] for j in (-1, 0, 1)]
        leonard = [product(a, b) - centre[a] * centre[b] for a, b in pairs]
        third = (leonard[0] + leonard[1] + leonard[2]) * (1.0 / 3.0)
        leonard = [x - third for x in leonard[:3]] + leonard[3:]
        model = [stress(k) - scale * s[k] for k in range(6)]
        lm = [x * y for x, y in zip(leonard, model)]
        mm = [x * x for x in model]
        num = (lm[0] + lm[1] + lm[2]) + 2.0 * (lm[3] + lm[4] + lm[5])
        den = (mm[0] + mm[1] + mm[2]) + 2.0 * (mm[3] + mm[4] + mm[5])
        return num, den

    def fold(value):
        parts = [value[:, k:k + 128] for k in range(0, value.shape[1], 128)]
        return functools.reduce(lambda x, y: x + y, parts)

    def sums(t, rows):
        both = [sums_row(t, row) for row in rows]
        num = functools.reduce(lambda x, y: x + y, [b[0] for b in both])
        den = functools.reduce(lambda x, y: x + y, [b[1] for b in both])
        accn[tile(t - 1), :] += fold(num)
        accd[tile(t - 1), :] += fold(den)

    open_round(0)

    def inner_filter(t, carry):
        span_rows(t, range(2, nx + 2))
        filtered_rows(t, range(3, nx + 1))
        return carry

    lax.fori_loop(0, nt + 2, inner_filter, 0)

    close_round(0)
    open_round(1)
    half = (nx - 2) // 2

    def inner_stress(i, carry):
        t = i // half + 1
        row = 3 + 2 * lax.rem(i, half)
        stress_row(t, row, True)
        stress_row(t, row + 1, True)
        return carry

    lax.fori_loop(0, nt * half, inner_stress, 0)

    close_round(1)
    open_round(2)

    def inner_sums(t, carry):
        sums(t, range(4, nx))
        return carry

    lax.fori_loop(1, nt + 1, inner_sums, 0)
    close_round(2)

    def later_round(k, carry):
        to_sides(ring.at[k])
        pl.semaphore_wait(ring.at[k], 2)
        return carry

    if rounds > 3:
        lax.fori_loop(3, rounds, later_round, 0)
    to_ends(ring.at[n // 2])

    def rim_first(t):
        span_rows(t, (0, nx + 3), False)
        span_rows(t, (1, nx + 2))
        filtered_rows(t, (1, 2, nx + 1, nx + 2))

    def rim_second(t):
        for row in (1, 2, nx + 1, nx + 2):
            stress_row(t, row, row in (2, nx + 1))
        sums(t, (2, 3, nx, nx + 1))

    def arrive(t):
        x_copy(0, t).wait_recv()
        x_copy(1, t).wait_recv()
        rim_first(t)

    def arrive_early(i, carry):
        arrive(jnp.where(i < 2, nt - i, i - 1))
        return carry

    lax.fori_loop(0, EARLY, arrive_early, 0)
    for side in range(2):
        c_copy(side).wait_recv()
    for side in range(2):
        dst = nx + 2 if side == 0 else 0
        for c in range(3):
            for r in range(2):
                k = 2 * c + r
                u[c, dst + r, 7:8, :] = edge_in[side, k:k + 1, :]
                u[c, dst + r, ny + 8:ny + 9, :] = edge_in[side, 6 + k:7 + k, :]

    def rim_ends(i, carry):
        rim_first(i * (nt + 1))
        return carry

    lax.fori_loop(0, 2, rim_ends, 0)

    def finish_ends(i, carry):
        rim_second(1 + i * (nt - 1))
        return carry

    lax.fori_loop(0, 2, finish_ends, 0)

    def column_sums(ref):
        ref[0:1, :] = jnp.sum(accn[...].T, axis=0, keepdims=True)
        ref[1:2, :] = jnp.sum(accd[...].T, axis=0, keepdims=True)

    def g_copy(kind, to_x, to_y):
        return pltpu.make_async_remote_copy(
            src_ref=mine if kind == 0 else mine_ends,
            dst_ref=gather.at[kind, gx],
            send_sem=g_send.at[kind],
            recv_sem=g_recv.at[kind],
            device_id=(to_x, to_y),
            device_id_type=MESH,
        )

    def g_all(kind):
        count = n - 1 if kind == 0 else n
        part = gather.at[kind, 0:count]
        return pltpu.make_async_remote_copy(
            src_ref=part,
            dst_ref=part,
            send_sem=g_send.at[kind],
            recv_sem=g_recv.at[kind],
            device_id=(right, gy),
            device_id_type=MESH,
        )

    column_sums(mine_ends)
    pl.semaphore_wait(ring.at[n // 2], ends)

    def send_ends(i, carry):
        @pl.when(not_low)
        def _():
            g_copy(2, i, gy - 1).start()

        @pl.when(not_high)
        def _():
            g_copy(1, i, gy + 1).start()

        return carry

    lax.fori_loop(0, n, send_ends, 0)

    def finish(t, carry):
        @pl.when(t < nt - 1)
        def _():
            arrive(t)

        rim_second(t - 1)
        return carry

    lax.fori_loop(EARLY - 1, nt - 1, finish, 0)

    def finish_last(i, carry):
        rim_second(nt - 2 + i)
        rim_second(nt - 1 + i)
        return carry

    lax.fori_loop(0, 1, finish_last, 0)

    column_sums(mine)

    def send(i, carry):
        g_copy(0, lax.rem(gx + i, n), gy).start()
        return carry

    lax.fori_loop(1, n, send, 0)
    gather[0, gx] = mine[...]
    g_all(0).wait_recv()

    @pl.when(not_low)
    def _():
        g_all(1).wait_recv()

    @pl.when(not_high)
    def _():
        g_all(2).wait_recv()

    def profile(kind):
        def add(i, total):
            return total + gather[kind, i]

        total = lax.fori_loop(0, n, add, jnp.zeros((2, lanes), jnp.float32))
        return jnp.clip(2.0 * (total[0:1] / total[1:2]), 0.0, clip_high)

    raw = profile(0)
    where = lax.broadcasted_iota(jnp.int32, (1, lanes), 1)
    first = where == 0
    last = where == ny - 1
    under = jnp.where(first, raw, pltpu.roll(raw, 1, 1))
    over = jnp.where(last, raw, pltpu.roll(raw, lanes - 1, 1))
    low_raw = pltpu.roll(profile(1), (lanes + 1 - ny) % lanes, 1)
    high_raw = pltpu.roll(profile(2), ny - 1, 1)
    under = jnp.where(jnp.logical_and(first, not_low), low_raw, under)
    over = jnp.where(jnp.logical_and(last, not_high), high_raw, over)
    coef_ref[...] = 0.25 * under + 0.5 * raw + 0.25 * over

    for side in range(2):
        x_all(side).wait_send()
    for side in range(2):
        c_copy(side).wait_send()

    @pl.when(not_low)
    def _():
        y_copy(0).wait_send()

    @pl.when(not_high)
    def _():
        y_copy(1).wait_send()

    g_all(0).wait_send()

    @pl.when(not_low)
    def _():
        g_all(2).wait_send()

    @pl.when(not_high)
    def _():
        g_all(1).wait_send()


def local(n, m, velocity):
    _, nx, ny, nz = velocity.shape
    lanes = -(-ny // 128) * 128
    nt = ny // 8
    f32 = jnp.float32
    strength, coef = pl.pallas_call(
        functools.partial(kernel, n, m, nx, ny),
        out_shape=(
            jax.ShapeDtypeStruct((nx, ny, nz), f32),
            jax.ShapeDtypeStruct((1, lanes), f32),
        ),
        in_specs=[pl.BlockSpec(memory_space=pltpu.HBM)],
        out_specs=(
            pl.BlockSpec(memory_space=pltpu.VMEM),
            pl.BlockSpec(memory_space=pltpu.VMEM),
        ),
        scratch_shapes=[
            pltpu.VMEM((3, nx + 4, ny + 16, nz), f32),
            pltpu.VMEM((3, nx + 4, ny + 16, nz), f32),
            pltpu.VMEM((3, nx + 4, ny + 16, nz), f32),
            pltpu.VMEM((3, nx + 4, ny + 16, nz), f32),
            pltpu.VMEM((6, nx + 4, ny, nz), f32),
            pltpu.VMEM((lanes, 128), f32),
            pltpu.VMEM((lanes, 128), f32),
            pltpu.VMEM((2, 12, nz), f32),
            pltpu.VMEM((2, 12, nz), f32),
            pltpu.VMEM((2, lanes), f32),
            pltpu.VMEM((2, lanes), f32),
            pltpu.VMEM((3, n, 2, lanes), f32),
            pltpu.SemaphoreType.DMA,
            pltpu.SemaphoreType.DMA((2,)),
            pltpu.SemaphoreType.DMA((2, nt)),
            pltpu.SemaphoreType.DMA((2,)),
            pltpu.SemaphoreType.DMA((2,)),
            pltpu.SemaphoreType.DMA((2,)),
            pltpu.SemaphoreType.DMA((2,)),
            pltpu.SemaphoreType.DMA((3,)),
            pltpu.SemaphoreType.DMA((3,)),
            pltpu.SemaphoreType.REGULAR((n // 2 + 1,)),
        ],
        compiler_params=pltpu.CompilerParams(
            collective_id=0, has_side_effects=True, vmem_limit_bytes=32 * 1024 * 1024
        ),
    )(pltpu.with_memory_space_constraint(velocity, pltpu.HBM))
    smooth = coef[0, :ny]
    return (smooth, smooth[None, :, None] * strength)


def solution(mesh):
    n, m = mesh.shape["gx"], mesh.shape["gy"]
    return jax.shard_map(
        functools.partial(local, n, m),
        mesh=mesh,
        in_specs=(P(None, "gx", "gy", None),),
        out_specs=(P("gy"), P("gx", "gy", None)),
        check_vma=False,
    )
```

profile of v0, /device:TPU:0, one launch (start us, length us, event | category | flops | bytes accessed | tf_op | source)
XLA Modules:
  0.0 31.8 jit_solution(3673461796983101625)
XLA Ops:
  0.6 30.2 %shard_map.30 = (f32[8,64,256]{2,1,0:T(8,128)S(1)}, f32[1,128]{1,0:T(1,128)S(1)}) custom-call(f32[3,8,64,256]{3,2,1,0:T(8,128)} %u_hbm.1), custom_call_target="tpu_custom_call" | custom-call | tf_op jit(solution)/shard_map/pallas_call | solution.py:466
  30.8 0.0 copy-start
  30.9 0.9 %broadcast_multiply_fusion = f32[8,64,256]{2,1,0:T(8,128)} fusion(f32[8,64,256]{2,1,0:T(8,128)S(1)} %get-tuple-element.5, f32[64]{0:T(128)S(1)} %slice_bitcast_fusion), kind=kLoop, calls=%fused_computation | loop fusion | flops 131072 | bytes 1048832 | tf_op jit(solution)/shard_map/mul | solution.py:506
  31.8 0.0 copy-done
  (1 shorter events, 0.0 us)
Async XLA Ops:
  30.8 0.9 %copy-start = (f32[64]{0:T(128)}, f32[64]{0:T(128)S(1)}, u32[]{:S(2)}) copy-start(f32[64]{0:T(128)S(1)} %slice_bitcast_fusion) | copy-start | bytes 772
where the time goes:
time: 31.9 us; the launch traced here: 31.8 us
  Pallas kernels  30.2 us (95%)
  other arithmetic  0.9 us (3%)
  between operations  0.65 us (2%)
    pallas_call x1, Pallas kernels, local(): pl.pallas_call(functools.partial(kernel, n, m, nx, ny), out_shape=(jax.Sh...  30.2 us
    mul x1, other arithmetic, local(): return (smooth, smooth[None, :, None] * strength)  0.9 us

commit v1 on v0

v1 whole, which is shorter than its diff:
```python
import functools

import jax
import jax.numpy as jnp
from jax import lax
from jax.experimental import pallas as pl
from jax.experimental.pallas import tpu as pltpu
from jax.sharding import PartitionSpec as P

clip_high = 0.1
pairs = ((0, 0), (1, 1), (2, 2), (0, 1), (0, 2), (1, 2))
MESH = pl.DeviceIdType.MESH
HALO = 3


def tile(index):
    return pl.ds(pl.multiple_of(index * 8, 8), 8)


def roll_next(value):
    return pltpu.roll(value, value.shape[1] - 1, 1)


def roll_prev(value):
    return pltpu.roll(value, 1, 1)


def filter_span(value):
    return (roll_next(value) + roll_prev(value)) + 2.0 * value


def slope_span(value):
    return roll_next(value) - roll_prev(value)


def slope_wall(ref, comp, row, t, here):
    rows = lax.broadcasted_iota(jnp.int32, here.shape, 0)
    below = ref[comp, row, tile(t - 1), :]
    above = ref[comp, row, tile(t + 1), :]
    up = pltpu.roll(jnp.where(rows == 0, above, here), 7, 0)
    down = pltpu.roll(jnp.where(rows == 7, below, here), 1, 0)
    return up - down


def strain4(ref, row, t, slope=None):
    here = [ref[c, row, tile(t), :] for c in range(3)]
    dx = [ref[c, row + 1, tile(t), :] - ref[c, row - 1, tile(t), :] for c in range(3)]
    dy = [slope_wall(ref, c, row, t, here[c]) for c in range(3)]
    if slope is None:
        dz = [slope_span(here[c]) for c in range(3)]
    else:
        dz = [slope[c, row, tile(t), :] for c in range(3)]
    s = (
        dx[0],
        4.0 * dy[1],
        2.0 * dz[2],
        2.0 * dy[0] + 0.5 * dx[1],
        dz[0] + 0.5 * dx[2],
        dz[1] + 2.0 * dy[2],
    )
    diag = s[0] * s[0] + s[1] * s[1] + s[2] * s[2]
    off = s[3] * s[3] + s[4] * s[4] + s[5] * s[5]
    return here, s, diag + 2.0 * off


def kernel(n, m, nx, ny, shifts, u_hbm, strength, coef_ref, u, w, v, d, g, accn, accd,
           mine, mine_ends, gather, own_sem, xs_send, xs_recv, ys_send, ys_recv,
           c_send, c_recv, g_send, g_recv, ready, ring):
    nt = ny // 8
    edge_lo, edge_hi = HALO, HALO + nx - 1
    gx = lax.axis_index("gx")
    gy = lax.axis_index("gy")
    left, right = lax.rem(gx + n - 1, n), lax.rem(gx + 1, n)
    not_low, not_high = gy > 0, gy < m - 1
    begins, ends_ring = gx == 0, gx == n - 1
    lanes = mine.shape[-1]
    shifting = any(shifts)

    def shift_at(index):
        value = jnp.int32(shifts[0])
        for i in range(1, n):
            if shifts[i] != shifts[0]:
                value = jnp.where(index == i, jnp.int32(shifts[i]), value)
        return value

    gains = (shift_at(left), -shift_at(gx)) if shifting else (0, 0)
    more = [jnp.maximum(x, 0) if shifting else 0 for x in gains]
    fewer = [jnp.maximum(-x, 0) if shifting else 0 for x in gains]

    own = [
        pltpu.make_async_copy(
            u_hbm.at[:, a:b, :, :], u.at[:, edge_lo + a:edge_lo + b, 8:8 + ny, :], own_sem.at[k]
        )
        for k, (a, b) in enumerate(((0, 1), (nx - 1, nx), (1, nx - 1)))
    ]
    for copy in own:
        copy.start()

    def signal(semaphore, to_x, to_y):
        pl.semaphore_signal(semaphore, inc=1, device_id=(to_x, to_y), device_id_type=MESH)

    barrier = pltpu.get_barrier_semaphore()

    @pl.when(jnp.logical_not(ends_ring))
    def _():
        signal(barrier, right, gy)

    @pl.when(begins)
    def _():
        signal(barrier, left, gy)

    @pl.when(not_high)
    def _():
        signal(barrier, gx, gy + 1)

    earlier = [jnp.where(x, 1, 0) for x in (gx > 0, ends_ring, not_low)]
    greeted = earlier[0] + earlier[1] + earlier[2]

    @pl.when(greeted > 0)
    def _():
        pl.semaphore_wait(barrier, greeted)

    @pl.when(gx > 0)
    def _():
        signal(ready.at[0], left, gy)

    @pl.when(ends_ring)
    def _():
        signal(ready.at[1], right, gy)

    @pl.when(not_low)
    def _():
        signal(ready.at[2], gx, gy - 1)

    ends = jnp.where(not_low, 1, 0) + jnp.where(not_high, 1, 0)
    rounds = n // 2 - 1

    def to_sides(semaphore):
        for side in (left, right):
            signal(semaphore, side, gy)

    def to_ends(semaphore):
        @pl.when(not_low)
        def _():
            signal(semaphore, gx, gy - 1)

        @pl.when(not_high)
        def _():
            signal(semaphore, gx, gy + 1)

    def open_round(k):
        if k < rounds:
            to_sides(ring.at[k])

    def close_round(k):
        if k < rounds:
            pl.semaphore_wait(ring.at[k], 2)

    def order(i):
        return jnp.where(i == 0, nt, i)

    def halo_row(side, k):
        return edge_lo - k if side == 0 else edge_hi + k

    def x_copy(side, k, t):
        src = halo_row(side, 1 - k)
        dst = halo_row(1 - side, k)
        return pltpu.make_async_remote_copy(
            src_ref=u.at[:, src:src + 1, tile(t), :],
            dst_ref=u.at[:, dst:dst + 1, tile(t), :],
            send_sem=xs_send.at[side, k - 1, t - 1],
            recv_sem=xs_recv.at[1 - side, k - 1, t - 1],
            device_id=(left if side == 0 else right, gy),
            device_id_type=MESH,
        )

    def all_sends(side, k, act):
        def each(i, carry):
            act(x_copy(side, k, order(i)))
            return carry

        low = nt - fewer[side] if k == 3 else 0
        high = nt - more[side] if k == 2 else nt
        if k < 3 or shifting:
            lax.fori_loop(low, high, each, 0)

    def send_x(side, k):
        all_sends(side, k, lambda copy: copy.start())

    def y_copy(side):
        src = 8 if side == 0 else ny
        dst = ny + 8 if side == 0 else 0
        return pltpu.make_async_remote_copy(
            src_ref=u.at[:, edge_lo:edge_lo + nx, src:src + 8, :],
            dst_ref=u.at[:, edge_lo:edge_lo + nx, dst:dst + 8, :],
            send_sem=ys_send.at[side],
            recv_sem=ys_recv.at[side],
            device_id=(gx, gy - 1 if side == 0 else gy + 1),
            device_id_type=MESH,
        )

    def c_copy(side, end):
        row = halo_row(side, 1)
        src = 8 if end == 0 else ny
        dst = ny + 8 if end == 0 else 0
        return pltpu.make_async_remote_copy(
            src_ref=u.at[:, row:row + 1, src:src + 8, :],
            dst_ref=u.at[:, row:row + 1, dst:dst + 8, :],
            send_sem=c_send.at[side, end],
            recv_sem=c_recv.at[side, end],
            device_id=(gx, gy - 1 if end == 0 else gy + 1),
            device_id_type=MESH,
        )

    own[0].wait()

    @pl.when(gx > 0)
    def _():
        send_x(0, 1)

    own[1].wait()

    @pl.when(ends_ring)
    def _():
        send_x(1, 1)

    own[2].wait()

    @pl.when(gx > 0)
    def _():
        send_x(0, 2)
        send_x(0, 3)

    @pl.when(ends_ring)
    def _():
        send_x(1, 2)
        send_x(1, 3)

    @pl.when(not_low)
    def _():
        y_copy(0).start()

    @pl.when(jnp.logical_not(ends_ring))
    def _():
        pl.semaphore_wait(ready.at[0], 1)
        for k in (1, 2, 3):
            send_x(1, k)

    @pl.when(not_high)
    def _():
        pl.semaphore_wait(ready.at[2], 1)
        y_copy(1).start()

    accn[...] = jnp.zeros_like(accn)
    accd[...] = jnp.zeros_like(accd)
    rows_all = u.shape[1]

    @pl.when(jnp.logical_not(not_low))
    def _():
        u[:, :, 0:8, :] = jnp.zeros((3, rows_all, 8, u.shape[3]), jnp.float32)

    @pl.when(jnp.logical_not(not_high))
    def _():
        u[:, :, ny + 8:ny + 16, :] = jnp.zeros((3, rows_all, 8, u.shape[3]), jnp.float32)

    def span_rows(t, rows, slopes=True):
        for c in range(3):
            for row in rows:
                here = u[c, row, tile(t), :]
                after, before = roll_next(here), roll_prev(here)
                w[c, row, tile(t), :] = (after + before) + 2.0 * here
                if slopes:
                    d[c, row, tile(t), :] = after - before

    def filtered_rows(t, rows):
        for c in range(3):
            for row in rows:
                a, b, e = (w[c, row + k, tile(t), :] for k in (-1, 0, 1))
                v[c, row, tile(t), :] = 0.25 * ((a + e) + 2.0 * b)

    def stress_row(t, row, keep):
        _, s, total = strain4(u, row, t, d)
        size = jnp.sqrt(0.125 * total)
        if keep:
            strength[row - edge_lo, tile(t - 1), :] = size
        for k in range(6):
            g[k, row, tile(t - 1), :] = size * s[k]

    def sums_row(t, row):
        centre, s, total = strain4(v, row, t)
        scale = jnp.sqrt(2.0 * total)

        def product(a, b):
            one, two, three = (near[j][a] * near[j][b] for j in range(3))
            return filter_span((one + three) + 2.0 * two)

        def stress(k):
            one, two, three = (g[k, row + j, tile(t - 1), :] for j in (-1, 0, 1))
            return filter_span((one + three) + 2.0 * two)

        near = [[u[c, row + j, tile(t), :] for c in range(3)] for j in (-1, 0, 1)]
        leonard = [product(a, b) - centre[a] * centre[b] for a, b in pairs]
        third = (leonard[0] + leonard[1] + leonard[2]) * (1.0 / 3.0)
        leonard = [x - third for x in leonard[:3]] + leonard[3:]
        model = [stress(k) - scale * s[k] for k in range(6)]
        lm = [x * y for x, y in zip(leonard, model)]
        mm = [x * x for x in model]
        num = (lm[0] + lm[1] + lm[2]) + 2.0 * (lm[3] + lm[4] + lm[5])
        den = (mm[0] + mm[1] + mm[2]) + 2.0 * (mm[3] + mm[4] + mm[5])
        return num, den

    def fold(value):
        parts = [value[:, k:k + 128] for k in range(0, value.shape[1], 128)]
        return functools.reduce(lambda x, y: x + y, parts)

    def sums(t, rows):
        both = [sums_row(t, row) for row in rows]
        num = functools.reduce(lambda x, y: x + y, [b[0] for b in both])
        den = functools.reduce(lambda x, y: x + y, [b[1] for b in both])
        accn[tile(t - 1), :] += fold(num)
        accd[tile(t - 1), :] += fold(den)

    def inner_filter(t, carry):
        span_rows(t, range(edge_lo, edge_hi + 1))
        filtered_rows(t, range(edge_lo + 1, edge_hi))
        return carry

    lax.fori_loop(1, nt + 1, inner_filter, 0)

    @pl.when(not_high)
    def _():
        y_copy(0).wait_recv()

    @pl.when(not_low)
    def _():
        y_copy(1).wait_recv()

    def end_filter(i, carry):
        return inner_filter(i * (nt + 1), carry)

    lax.fori_loop(0, 2, end_filter, 0)

    half = (nx - 2) // 2

    def inner_stress(i, carry):
        t = i // half + 1
        row = edge_lo + 1 + 2 * lax.rem(i, half)
        stress_row(t, row, True)
        stress_row(t, row + 1, True)
        return carry

    lax.fori_loop(0, nt * half, inner_stress, 0)

    def inner_sums(t, carry):
        sums(t, range(edge_lo + 2, edge_hi - 1))
        return carry

    lax.fori_loop(1, nt + 1, inner_sums, 0)

    @pl.when(begins)
    def _():
        pl.semaphore_wait(ready.at[1], 1)
        for k in (1, 2, 3):
            send_x(0, k)

    open_round(0)

    def step(side, k, t):
        x_copy(1 - side, k, t).wait_recv()
        new, middle, old = (halo_row(side, k - j) for j in range(3))
        span_rows(t, (new,), k == 1 or shifting and k == 2)
        filtered_rows(t, (middle,))
        stress_row(t, middle, k == 1)
        sums(t, (old,))

    def near(i, carry):
        t = order(i)
        for side in range(2):
            step(side, 1, t)

            @pl.when(jnp.logical_and(i == 0, not_high))
            def _():
                c_copy(side, 1).start()

            @pl.when(jnp.logical_and(i == 1, not_low))
            def _():
                c_copy(side, 0).start()

        return carry

    lax.fori_loop(0, nt, near, 0)
    close_round(0)
    open_round(1)

    for side in range(2):
        @pl.when(not_high)
        def _():
            c_copy(side, 0).wait_recv()

        @pl.when(not_low)
        def _():
            c_copy(side, 1).wait_recv()

    def corners(i, carry):
        t = i * (nt + 1)
        for side in range(2):
            span_rows(t, (halo_row(side, 1),), False)
            filtered_rows(t, (halo_row(side, 0),))
        return carry

    lax.fori_loop(0, 2, corners, 0)
    close_round(1)
    open_round(2)

    def far(k):
        def run(i, carry):
            t = order(i)
            for side in range(2):
                if not shifting:
                    step(side, k, t)
                    continue
                wanted = i < nt - fewer[side] if k == 2 else i >= nt - more[side]

                @pl.when(wanted)
                def _():
                    step(side, k, t)

            return carry

        return run

    lax.fori_loop(0, 2, far(2), 0)
    close_round(2)

    def later_round(k, carry):
        to_sides(ring.at[k])
        pl.semaphore_wait(ring.at[k], 2)
        return carry

    if rounds > 3:
        lax.fori_loop(3, rounds, later_round, 0)
    to_ends(ring.at[n // 2])

    def column_sums(ref):
        ref[0:1, :] = jnp.sum(accn[...].T, axis=0, keepdims=True)
        ref[1:2, :] = jnp.sum(accd[...].T, axis=0, keepdims=True)

    def g_copy(kind, to_x, to_y):
        return pltpu.make_async_remote_copy(
            src_ref=mine if kind == 0 else mine_ends,
            dst_ref=gather.at[kind, gx],
            send_sem=g_send.at[kind],
            recv_sem=g_recv.at[kind],
            device_id=(to_x, to_y),
            device_id_type=MESH,
        )

    def g_all(kind):
        count = n - 1 if kind == 0 else n
        part = gather.at[kind, 0:count]
        return pltpu.make_async_remote_copy(
            src_ref=part,
            dst_ref=part,
            send_sem=g_send.at[kind],
            recv_sem=g_recv.at[kind],
            device_id=(right, gy),
            device_id_type=MESH,
        )

    column_sums(mine_ends)
    pl.semaphore_wait(ring.at[n // 2], ends)

    def send_ends(i, carry):
        @pl.when(not_low)
        def _():
            g_copy(2, i, gy - 1).start()

        @pl.when(not_high)
        def _():
            g_copy(1, i, gy + 1).start()

        return carry

    lax.fori_loop(0, n, send_ends, 0)

    lax.fori_loop(2, nt, far(2), 0)
    if shifting:
        top = functools.reduce(jnp.maximum, more)
        lax.fori_loop(nt - top, nt, far(3), 0)

    column_sums(mine)
    def drain():
        for side in range(2):
            for k in (1, 2, 3):
                all_sends(side, k, lambda copy: copy.wait_send())

    def send(i, carry):
        g_copy(0, lax.rem(gx + i, n), gy).start()
        return carry

    lax.fori_loop(1, n, send, 0)
    gather[0, gx] = mine[...]
    drain()
    g_all(0).wait_recv()

    @pl.when(not_low)
    def _():
        g_all(1).wait_recv()

    @pl.when(not_high)
    def _():
        g_all(2).wait_recv()

    def profile(kind):
        def add(i, total):
            return total + gather[kind, i]

        total = lax.fori_loop(0, n, add, jnp.zeros((2, lanes), jnp.float32))
        return jnp.clip(2.0 * (total[0:1] / total[1:2]), 0.0, clip_high)

    raw = profile(0)
    where = lax.broadcasted_iota(jnp.int32, (1, lanes), 1)
    first = where == 0
    last = where == ny - 1
    under = jnp.where(first, raw, pltpu.roll(raw, 1, 1))
    over = jnp.where(last, raw, pltpu.roll(raw, lanes - 1, 1))
    low_raw = pltpu.roll(profile(1), (lanes + 1 - ny) % lanes, 1)
    high_raw = pltpu.roll(profile(2), ny - 1, 1)
    under = jnp.where(jnp.logical_and(first, not_low), low_raw, under)
    over = jnp.where(jnp.logical_and(last, not_high), high_raw, over)
    coef_ref[...] = 0.25 * under + 0.5 * raw + 0.25 * over

    for side in range(2):
        @pl.when(not_low)
        def _():
            c_copy(side, 0).wait_send()

        @pl.when(not_high)
        def _():
            c_copy(side, 1).wait_send()

    @pl.when(not_low)
    def _():
        y_copy(0).wait_send()

    @pl.when(not_high)
    def _():
        y_copy(1).wait_send()

    g_all(0).wait_send()

    @pl.when(not_low)
    def _():
        g_all(2).wait_send()

    @pl.when(not_high)
    def _():
        g_all(1).wait_send()


def local(n, m, shifts, velocity):
    _, nx, ny, nz = velocity.shape
    lanes = -(-ny // 128) * 128
    nt = ny // 8
    f32 = jnp.float32
    strength, coef = pl.pallas_call(
        functools.partial(kernel, n, m, nx, ny, shifts),
        out_shape=(
            jax.ShapeDtypeStruct((nx, ny, nz), f32),
            jax.ShapeDtypeStruct((1, lanes), f32),
        ),
        in_specs=[pl.BlockSpec(memory_space=pltpu.HBM)],
        out_specs=(
            pl.BlockSpec(memory_space=pltpu.VMEM),
            pl.BlockSpec(memory_space=pltpu.VMEM),
        ),
        scratch_shapes=[
            pltpu.VMEM((3, nx + 2 * HALO, ny + 16, nz), f32),
            pltpu.VMEM((3, nx + 2 * HALO, ny + 16, nz), f32),
            pltpu.VMEM((3, nx + 2 * HALO, ny + 16, nz), f32),
            pltpu.VMEM((3, nx + 2 * HALO, ny + 16, nz), f32),
            pltpu.VMEM((6, nx + 2 * HALO, ny, nz), f32),
            pltpu.VMEM((lanes, 128), f32),
            pltpu.VMEM((lanes, 128), f32),
            pltpu.VMEM((2, lanes), f32),
            pltpu.VMEM((2, lanes), f32),
            pltpu.VMEM((3, n, 2, lanes), f32),
            pltpu.SemaphoreType.DMA((3,)),
            pltpu.SemaphoreType.DMA((2, HALO, nt)),
            pltpu.SemaphoreType.DMA((2, HALO, nt)),
            pltpu.SemaphoreType.DMA((2,)),
            pltpu.SemaphoreType.DMA((2,)),
            pltpu.SemaphoreType.DMA((2, 2)),
            pltpu.SemaphoreType.DMA((2, 2)),
            pltpu.SemaphoreType.DMA((3,)),
            pltpu.SemaphoreType.DMA((3,)),
            pltpu.SemaphoreType.REGULAR((3,)),
            pltpu.SemaphoreType.REGULAR((n // 2 + 1,)),
        ],
        compiler_params=pltpu.CompilerParams(
            collective_id=0, has_side_effects=True, vmem_limit_bytes=32 * 1024 * 1024
        ),
    )(pltpu.with_memory_space_constraint(velocity, pltpu.HBM))
    smooth = coef[0, :ny]
    return (smooth, smooth[None, :, None] * strength)


def solution(mesh):
    n, m = mesh.shape["gx"], mesh.shape["gy"]
    shifts = (0,) * n
    return jax.shard_map(
        functools.partial(local, n, m, shifts),
        mesh=mesh,
        in_specs=(P(None, "gx", "gy", None),),
        out_specs=(P("gy"), P("gx", "gy", None)),
        check_vma=False,
    )
```

time: 31.9 us -> 33.3 us (1.044); the launches traced: 31.8 us -> 32.7 us
  Pallas kernels: 30.2 us -> 31.1 us
    pallas_call x1, Pallas kernels: 30.2 us -> 31.1 us  [local(): pl.pallas_call(functools.partial(kernel, n, m, nx, ny, shifts), out_shape...]
where the time goes in v1:
time: 33.3 us; the launch traced here: 32.7 us
  Pallas kernels  31.1 us (93%)
  other arithmetic  0.9 us (3%)
  between operations  0.65 us (2%)
    pallas_call x1, Pallas kernels, local(): pl.pallas_call(functools.partial(kernel, n, m, nx, ny, shifts), out_shape...  31.1 us
    mul x1, other arithmetic, local(): return (smooth, smooth[None, :, None] * strength)  0.9 us

profile of v1, /device:TPU:0, one launch (start us, length us, event | category | flops | bytes accessed | tf_op | source)
XLA Modules:
  0.0 32.7 jit_solution(5686729296412682936)
XLA Ops:
  0.6 31.1 %shard_map.30 = (f32[8,64,256]{2,1,0:T(8,128)S(1)}, f32[1,128]{1,0:T(1,128)S(1)}) custom-call(f32[3,8,64,256]{3,2,1,0:T(8,128)} %u_hbm.1), custom_call_target="tpu_custom_call" | custom-call | tf_op jit(solution)/shard_map/pallas_call | solution.py:566
  31.8 0.0 copy-start
  31.8 0.9 %broadcast_multiply_fusion = f32[8,64,256]{2,1,0:T(8,128)} fusion(f32[8,64,256]{2,1,0:T(8,128)S(1)} %get-tuple-element.5, f32[64]{0:T(128)S(1)} %slice_bitcast_fusion), kind=kLoop, calls=%fused_computation | loop fusion | flops 131072 | bytes 1048832 | tf_op jit(solution)/shard_map/mul | solution.py:605
  32.7 0.0 copy-done
  (1 shorter events, 0.0 us)
Async XLA Ops:
  31.8 0.9 %copy-start = (f32[64]{0:T(128)}, f32[64]{0:T(128)S(1)}, u32[]{:S(2)}) copy-start(f32[64]{0:T(128)S(1)} %slice_bitcast_fusion) | copy-start | bytes 772

commit v2 on v1

--- a/solution.py
+++ b/solution.py
@@ -63,18 +63,30 @@
     return here, s, diag + 2.0 * off
 
 
+def cuts_of(nt):
+    edges = [0, min(3, nt)]
+    while nt - edges[-1] > 1:
+        edges.append(min(edges[-1] + 2, nt - 1))
+    if edges[-1] < nt:
+        edges.append(nt)
+    return edges
+
+
 def kernel(n, m, nx, ny, shifts, u_hbm, strength, coef_ref, u, w, v, d, g, accn, accd,
-           mine, mine_ends, gather, own_sem, xs_send, xs_recv, ys_send, ys_recv,
-           c_send, c_recv, g_send, g_recv, ready, ring):
+           mine, mine_ends, gather, own_sem, xs_send, xs_recv, y_send, y_recv,
+           c_recv, g_send, g_recv, ready, ring):
     nt = ny // 8
     edge_lo, edge_hi = HALO, HALO + nx - 1
     gx = lax.axis_index("gx")
     gy = lax.axis_index("gy")
     left, right = lax.rem(gx + n - 1, n), lax.rem(gx + 1, n)
     not_low, not_high = gy > 0, gy < m - 1
-    begins, ends_ring = gx == 0, gx == n - 1
+    begins, closes = gx == 0, gx == n - 1
     lanes = mine.shape[-1]
     shifting = any(shifts)
+    cuts = cuts_of(nt)
+    pieces = len(cuts) - 1
+    moved = cuts[max(pieces - 2, 1)]
 
     def shift_at(index):
         value = jnp.int32(shifts[0])
@@ -84,8 +96,6 @@
         return value
 
     gains = (shift_at(left), -shift_at(gx)) if shifting else (0, 0)
-    more = [jnp.maximum(x, 0) if shifting else 0 for x in gains]
-    fewer = [jnp.maximum(-x, 0) if shifting else 0 for x in gains]
 
     own = [
         pltpu.make_async_copy(
@@ -101,7 +111,7 @@
 
     barrier = pltpu.get_barrier_semaphore()
 
-    @pl.when(jnp.logical_not(ends_ring))
+    @pl.when(jnp.logical_not(closes))
     def _():
         signal(barrier, right, gy)
 
@@ -113,7 +123,7 @@
     def _():
         signal(barrier, gx, gy + 1)
 
-    earlier = [jnp.where(x, 1, 0) for x in (gx > 0, ends_ring, not_low)]
+    earlier = [jnp.where(x, 1, 0) for x in (gx > 0, closes, not_low)]
     greeted = earlier[0] + earlier[1] + earlier[2]
 
     @pl.when(greeted > 0)
@@ -124,7 +134,7 @@
     def _():
         signal(ready.at[0], left, gy)
 
-    @pl.when(ends_ring)
+    @pl.when(closes)
     def _():
         signal(ready.at[1], right, gy)
 
@@ -133,11 +143,26 @@
         signal(ready.at[2], gx, gy - 1)
 
     ends = jnp.where(not_low, 1, 0) + jnp.where(not_high, 1, 0)
-    rounds = n // 2 - 1
-
-    def to_sides(semaphore):
-        for side in (left, right):
-            signal(semaphore, side, gy)
+    reaches = [2 ** k for k in range(n.bit_length()) if 2 ** k < n]
+
+    def open_round(k):
+        if k < len(reaches):
+            @pl.when(gx >= reaches[k])
+            def _():
+                signal(ring.at[k], gx - reaches[k], gy)
+
+            @pl.when(gx < n - reaches[k])
+            def _():
+                signal(ring.at[k], gx + reaches[k], gy)
+
+    def close_round(k):
+        if k < len(reaches):
+            near = (gx >= reaches[k], gx < n - reaches[k])
+            count = jnp.where(near[0], 1, 0) + jnp.where(near[1], 1, 0)
+
+            @pl.when(count > 0)
+            def _():
+                pl.semaphore_wait(ring.at[k], count)
 
     def to_ends(semaphore):
         @pl.when(not_low)
@@ -148,103 +173,158 @@
         def _():
             signal(semaphore, gx, gy + 1)
 
-    def open_round(k):
-        if k < rounds:
-            to_sides(ring.at[k])
-
-    def close_round(k):
-        if k < rounds:
-            pl.semaphore_wait(ring.at[k], 2)
-
     def order(i):
         return jnp.where(i == 0, nt, i)
 
     def halo_row(side, k):
         return edge_lo - k if side == 0 else edge_hi + k
 
-    def x_copy(side, k, t):
+    def x_copy(side, k, low, high, slot):
         src = halo_row(side, 1 - k)
         dst = halo_row(1 - side, k)
         return pltpu.make_async_remote_copy(
-            src_ref=u.at[:, src:src + 1, tile(t), :],
-            dst_ref=u.at[:, dst:dst + 1, tile(t), :],
-            send_sem=xs_send.at[side, k - 1, t - 1],
-            recv_sem=xs_recv.at[1 - side, k - 1, t - 1],
+            src_ref=u.at[:, src:src + 1, 8 * low:8 * high, :],
+            dst_ref=u.at[:, dst:dst + 1, 8 * low:8 * high, :],
+            send_sem=xs_send.at[side],
+            recv_sem=xs_recv.at[1 - side, slot],
             device_id=(left if side == 0 else right, gy),
             device_id_type=MESH,
         )
 
-    def all_sends(side, k, act):
-        def each(i, carry):
-            act(x_copy(side, k, order(i)))
-            return carry
-
-        low = nt - fewer[side] if k == 3 else 0
-        high = nt - more[side] if k == 2 else nt
-        if k < 3 or shifting:
-            lax.fori_loop(low, high, each, 0)
-
-    def send_x(side, k):
-        all_sends(side, k, lambda copy: copy.start())
+    def near_copy(side):
+        return x_copy(side, 1, 1, nt + 1, 0)
+
+    def moved_copy(side):
+        return x_copy(side, 3, moved, nt, pieces + 1)
+
+    def far_parts(p):
+        if p == 0:
+            return [(nt, nt + 1), (1, cuts[1])] if cuts[1] > 1 else [(nt, nt + 1)]
+        return [(cuts[p], cuts[p + 1])]
+
+    def start_far(side, p):
+        def run():
+            for low, high in far_parts(p):
+                x_copy(side, 2, low, high, p + 1).start()
+
+        if shifting and p >= pieces - 2:
+            pl.when(gains[side] <= 0)(run)
+        else:
+            run()
+
+    def start_moved(side):
+        if shifting:
+            @pl.when(gains[side] < 0)
+            def _():
+                moved_copy(side).start()
+
+    def wait_far(side, p):
+        count = cuts[p + 1] - cuts[p]
+        x_copy(1 - side, 2, 1, 1 + count, p + 1).wait_recv()
+
+    def tiles_view(count):
+        rows = next(r for r in range(1, u.shape[1] + 1) if count % r == 0 and count // r <= nt + 2)
+        return u.at[:, 0:rows, 0:8 * (count // rows), :]
+
+    def drain():
+        for side in range(2):
+            if not shifting:
+                wait_rows(side, tiles_view(nt))
+                continue
+            for sign, count in ((0, nt), (1, moved), (-1, 2 * nt - moved)):
+                @pl.when(gains[side] == sign)
+                def _():
+                    wait_rows(side, tiles_view(count))
 
     def y_copy(side):
-        src = 8 if side == 0 else ny
-        dst = ny + 8 if side == 0 else 0
+        src = 8 if side == 0 else ny + 7
+        dst = ny + 8 if side == 0 else 7
         return pltpu.make_async_remote_copy(
-            src_ref=u.at[:, edge_lo:edge_lo + nx, src:src + 8, :],
-            dst_ref=u.at[:, edge_lo:edge_lo + nx, dst:dst + 8, :],
-            send_sem=ys_send.at[side],
-            recv_sem=ys_recv.at[side],
+            src_ref=u.at[:, edge_lo:edge_lo + nx, src:src + 1, :],
+            dst_ref=u.at[:, edge_lo:edge_lo + nx, dst:dst + 1, :],
+            send_sem=y_send.at[side],
+            recv_sem=y_recv.at[side],
             device_id=(gx, gy - 1 if side == 0 else gy + 1),
             device_id_type=MESH,
         )
 
     def c_copy(side, end):
         row = halo_row(side, 1)
-        src = 8 if end == 0 else ny
-        dst = ny + 8 if end == 0 else 0
+        src = 8 if end == 0 else ny + 7
+        dst = ny + 8 if end == 0 else 7
         return pltpu.make_async_remote_copy(
-            src_ref=u.at[:, row:row + 1, src:src + 8, :],
-            dst_ref=u.at[:, row:row + 1, dst:dst + 8, :],
-            send_sem=c_send.at[side, end],
-            recv_sem=c_recv.at[side, end],
+            src_ref=u.at[:, row:row + 1, src:src + 1, :],
+            dst_ref=u.at[:, row:row + 1, dst:dst + 1, :],
+            send_sem=y_send.at[end],
+            recv_sem=c_recv.at[end],
             device_id=(gx, gy - 1 if end == 0 else gy + 1),
             device_id_type=MESH,
         )
 
+    def c_all(end, rows, semaphore):
+        part = u.at[:, 0:rows, 8:9, :]
+        return pltpu.make_async_remote_copy(
+            src_ref=part,
+            dst_ref=part,
+            send_sem=y_send.at[end],
+            recv_sem=semaphore,
+            device_id=(gx, gy - 1 if end == 0 else gy + 1),
+            device_id_type=MESH,
+        )
+
+    def wait_rows(side, part):
+        pltpu.make_async_remote_copy(
+            src_ref=part,
+            dst_ref=part,
+            send_sem=xs_send.at[side],
+            recv_sem=xs_recv.at[1 - side, 0],
+            device_id=(left if side == 0 else right, gy),
+            device_id_type=MESH,
+        ).wait_send()
+
+    plans = (((0, 1, 2, 3), (), (), (), ()), ((), (), (0, 1, 2, 3), (), ()))
+    odd = lax.rem(gy, 2) == 1
+
+    def start_all(point, sides=(0, 1)):
+        chosen = [[p for p in plan[point] if p < pieces] for plan in plans]
+
+        def run(parts):
+            for p in parts:
+                for side in sides:
+                    start_far(side, p)
+
+        if chosen[0] == chosen[1]:
+            run(chosen[0])
+            return
+        if chosen[0]:
+            pl.when(jnp.logical_not(odd))(lambda: run(chosen[0]))
+        if chosen[1]:
+            pl.when(odd)(lambda: run(chosen[1]))
+
     own[0].wait()
 
     @pl.when(gx > 0)
     def _():
-        send_x(0, 1)
+        near_copy(0).start()
 
     own[1].wait()
 
-    @pl.when(ends_ring)
-    def _():
-        send_x(1, 1)
+    @pl.when(closes)
+    def _():
+        near_copy(1).start()
 
     own[2].wait()
 
-    @pl.when(gx > 0)
-    def _():
-        send_x(0, 2)
-        send_x(0, 3)
-
-    @pl.when(ends_ring)
-    def _():
-        send_x(1, 2)
-        send_x(1, 3)
-
     @pl.when(not_low)
     def _():
         y_copy(0).start()
 
-    @pl.when(jnp.logical_not(ends_ring))
+    @pl.when(jnp.logical_not(closes))
     def _():
         pl.semaphore_wait(ready.at[0], 1)
-        for k in (1, 2, 3):
-            send_x(1, k)
+        near_copy(1).start()
+
+    open_round(0)
 
     @pl.when(not_high)
     def _():
@@ -350,56 +430,76 @@
         return carry
 
     lax.fori_loop(0, nt * half, inner_stress, 0)
+    close_round(0)
+    open_round(1)
+
+    @pl.when(begins)
+    def _():
+        pl.semaphore_wait(ready.at[1], 1)
+        near_copy(0).start()
 
     def inner_sums(t, carry):
         sums(t, range(edge_lo + 2, edge_hi - 1))
         return carry
 
     lax.fori_loop(1, nt + 1, inner_sums, 0)
-
-    @pl.when(begins)
-    def _():
-        pl.semaphore_wait(ready.at[1], 1)
-        for k in (1, 2, 3):
-            send_x(0, k)
-
-    open_round(0)
+    close_round(1)
+    open_round(2)
+
+    for side in range(2):
+        near_copy(side).wait_send()
+        start_all(0, (side,))
+
 
     def step(side, k, t):
-        x_copy(1 - side, k, t).wait_recv()
         new, middle, old = (halo_row(side, k - j) for j in range(3))
         span_rows(t, (new,), k == 1 or shifting and k == 2)
         filtered_rows(t, (middle,))
         stress_row(t, middle, k == 1)
         sums(t, (old,))
 
-    def near(i, carry):
-        t = order(i)
-        for side in range(2):
-            step(side, 1, t)
-
-            @pl.when(jnp.logical_and(i == 0, not_high))
-            def _():
-                c_copy(side, 1).start()
-
-            @pl.when(jnp.logical_and(i == 1, not_low))
-            def _():
-                c_copy(side, 0).start()
-
-        return carry
-
-    lax.fori_loop(0, nt, near, 0)
-    close_round(0)
-    open_round(1)
-
     for side in range(2):
+        near_copy(1 - side).wait_recv()
+
         @pl.when(not_high)
         def _():
-            c_copy(side, 0).wait_recv()
+            c_copy(side, 1).start()
 
         @pl.when(not_low)
         def _():
-            c_copy(side, 1).wait_recv()
+            c_copy(side, 0).start()
+
+    def near(i, carry):
+        for side in range(2):
+            step(side, 1, i)
+
+        @pl.when(i == nt // 2)
+        def _():
+            start_all(1)
+
+        return carry
+
+    lax.fori_loop(1, nt + 1, near, 0)
+    start_all(2)
+    for side in range(2):
+        start_moved(side)
+    close_round(2)
+
+    def later_round(k):
+        open_round(k)
+        close_round(k)
+
+    for k in range(3, len(reaches)):
+        later_round(k)
+    to_ends(ring.at[len(reaches)])
+
+    @pl.when(not_high)
+    def _():
+        c_all(0, 2, c_recv.at[0]).wait_recv()
+
+    @pl.when(not_low)
+    def _():
+        c_all(1, 2, c_recv.at[1]).wait_recv()
 
     def corners(i, carry):
         t = i * (nt + 1)
@@ -409,37 +509,33 @@
         return carry
 
     lax.fori_loop(0, 2, corners, 0)
-    close_round(1)
-    open_round(2)
-
-    def far(k):
-        def run(i, carry):
-            t = order(i)
+
+    def far(p):
+        def both(i, carry):
             for side in range(2):
-                if not shifting:
-                    step(side, k, t)
-                    continue
-                wanted = i < nt - fewer[side] if k == 2 else i >= nt - more[side]
-
-                @pl.when(wanted)
-                def _():
-                    step(side, k, t)
-
+                step(side, 2, order(i))
             return carry
 
-        return run
-
-    lax.fori_loop(0, 2, far(2), 0)
-    close_round(2)
-
-    def later_round(k, carry):
-        to_sides(ring.at[k])
-        pl.semaphore_wait(ring.at[k], 2)
-        return carry
-
-    if rounds > 3:
-        lax.fori_loop(3, rounds, later_round, 0)
-    to_ends(ring.at[n // 2])
+        def one(side):
+            def run(i, carry):
+                step(side, 2, order(i))
+                return carry
+
+            return run
+
+        if not shifting or p < pieces - 2:
+            for side in range(2):
+                wait_far(side, p)
+            lax.fori_loop(cuts[p], cuts[p + 1], both, 0)
+            return
+        for side in range(2):
+            @pl.when(gains[side] >= 0)
+            def _():
+                wait_far(side, p)
+                lax.fori_loop(cuts[p], cuts[p + 1], one(side), 0)
+
+    far(0)
+    start_all(3)
 
     def column_sums(ref):
         ref[0:1, :] = jnp.sum(accn[...].T, axis=0, keepdims=True)
@@ -468,7 +564,7 @@
         )
 
     column_sums(mine_ends)
-    pl.semaphore_wait(ring.at[n // 2], ends)
+    pl.semaphore_wait(ring.at[len(reaches)], ends)
 
     def send_ends(i, carry):
         @pl.when(not_low)
@@ -483,79 +579,75 @@
 
     lax.fori_loop(0, n, send_ends, 0)
 
-    lax.fori_loop(2, nt, far(2), 0)
+    for p in range(1, pieces):
+        far(p)
+        if p == 1:
+            start_all(4)
     if shifting:
-        top = functools.reduce(jnp.maximum, more)
-        lax.fori_loop(nt - top, nt, far(3), 0)
+        for side in range(2):
+            def run(i, carry):
+                step(side, 3, i)
+                return carry
+
+            @pl.when(gains[side] > 0)
+            def _():
+                moved_copy(1 - side).wait_recv()
+                lax.fori_loop(moved, nt, run, 0)
 
     column_sums(mine)
-    def drain():
-        for side in range(2):
-            for k in (1, 2, 3):
-                all_sends(side, k, lambda copy: copy.wait_send())
 
     def send(i, carry):
-        g_copy(0, lax.rem(gx + i, n), gy).start()
+        @pl.when(i != gx)
+        def _():
+            g_copy(0, i, gy).start()
+
         return carry
 
-    lax.fori_loop(1, n, send, 0)
+    lax.fori_loop(0, n, send, 0)
     gather[0, gx] = mine[...]
     drain()
+
+    @pl.when(not_low)
+    def _():
+        c_all(0, nx + 2, c_recv.at[0]).wait_send()
+
+    @pl.when(not_high)
+    def _():
+        c_all(1, nx + 2, c_recv.at[1]).wait_send()
+
+    @pl.when(not_low)
+    def _():
+        g_all(2).wait_send()
+
+    @pl.when(not_high)
+    def _():
+        g_all(1).wait_send()
+
+    @pl.when(not_low)
+    def _():
+        g_all(1).wait_recv()
+
+    @pl.when(not_high)
+    def _():
+        g_all(2).wait_recv()
+
+    def profile(kind):
+        total = functools.reduce(lambda x, y: x + y, [gather[kind, i] for i in range(n)])
+        return jnp.clip(2.0 * (total[0:1] / total[1:2]), 0.0, clip_high)
+
+    low_raw = pltpu.roll(profile(1), (lanes + 1 - ny) % lanes, 1)
+    high_raw = pltpu.roll(profile(2), ny - 1, 1)
     g_all(0).wait_recv()
-
-    @pl.when(not_low)
-    def _():
-        g_all(1).wait_recv()
-
-    @pl.when(not_high)
-    def _():
-        g_all(2).wait_recv()
-
-    def profile(kind):
-        def add(i, total):
-            return total + gather[kind, i]
-
-        total = lax.fori_loop(0, n, add, jnp.zeros((2, lanes), jnp.float32))
-        return jnp.clip(2.0 * (total[0:1] / total[1:2]), 0.0, clip_high)
-
     raw = profile(0)
     where = lax.broadcasted_iota(jnp.int32, (1, lanes), 1)
     first = where == 0
     last = where == ny - 1
     under = jnp.where(first, raw, pltpu.roll(raw, 1, 1))
     over = jnp.where(last, raw, pltpu.roll(raw, lanes - 1, 1))
-    low_raw = pltpu.roll(profile(1), (lanes + 1 - ny) % lanes, 1)
-    high_raw = pltpu.roll(profile(2), ny - 1, 1)
     under = jnp.where(jnp.logical_and(first, not_low), low_raw, under)
     over = jnp.where(jnp.logical_and(last, not_high), high_raw, over)
     coef_ref[...] = 0.25 * under + 0.5 * raw + 0.25 * over
-
-    for side in range(2):
-        @pl.when(not_low)
-        def _():
-            c_copy(side, 0).wait_send()
-
-        @pl.when(not_high)
-        def _():
-            c_copy(side, 1).wait_send()
-
-    @pl.when(not_low)
-    def _():
-        y_copy(0).wait_send()
-
-    @pl.when(not_high)
-    def _():
-        y_copy(1).wait_send()
-
     g_all(0).wait_send()
-
-    @pl.when(not_low)
-    def _():
-        g_all(2).wait_send()
-
-    @pl.when(not_high)
-    def _():
-        g_all(1).wait_send()
 
 
 def local(n, m, shifts, velocity):
@@ -586,16 +678,15 @@
             pltpu.VMEM((2, lanes), f32),
             pltpu.VMEM((3, n, 2, lanes), f32),
             pltpu.SemaphoreType.DMA((3,)),
-            pltpu.SemaphoreType.DMA((2, HALO, nt)),
-            pltpu.SemaphoreType.DMA((2, HALO, nt)),
+            pltpu.SemaphoreType.DMA((2,)),
+            pltpu.SemaphoreType.DMA((2, len(cuts_of(nt)) + (1 if any(shifts) else 0))),
             pltpu.SemaphoreType.DMA((2,)),
             pltpu.SemaphoreType.DMA((2,)),
-            pltpu.SemaphoreType.DMA((2, 2)),
-            pltpu.SemaphoreType.DMA((2, 2)),
+            pltpu.SemaphoreType.DMA((2,)),
             pltpu.SemaphoreType.DMA((3,)),
             pltpu.SemaphoreType.DMA((3,)),
             pltpu.SemaphoreType.REGULAR((3,)),
-            pltpu.SemaphoreType.REGULAR((n // 2 + 1,)),
+            pltpu.SemaphoreType.REGULAR((n.bit_length() + 1,)),
         ],
         compiler_params=pltpu.CompilerParams(
             collective_id=0, has_side_effects=True, vmem_limit_bytes=32 * 1024 * 1024
@@ -607,7 +698,7 @@
 
 def solution(mesh):
     n, m = mesh.shape["gx"], mesh.shape["gy"]
-    shifts = (0,) * n
+    shifts = (0,)*n
     return jax.shard_map(
         functools.partial(local, n, m, shifts),
         mesh=mesh,

time: 33.3 us -> 30.1 us (0.904); the launches traced: 32.7 us -> 29.9 us
  Pallas kernels: 31.1 us -> 28.4 us
    pallas_call x1, Pallas kernels: 31.1 us -> 28.4 us  [local(): pl.pallas_call(functools.partial(kernel, n, m, nx, ny, shifts), out_shape...]
where the time goes in v2:
time: 30.1 us; the launch traced here: 29.9 us
  Pallas kernels  28.4 us (94%)
  other arithmetic  0.9 us (3%)
  between operations  0.65 us (2%)
    pallas_call x1, Pallas kernels, local(): pl.pallas_call(functools.partial(kernel, n, m, nx, ny, shifts), out_shape...  28.4 us
    mul x1, other arithmetic, local(): return (smooth, smooth[None, :, None] * strength)  0.9 us

profile of v2, /device:TPU:0, one launch (start us, length us, event | category | flops | bytes accessed | tf_op | source)
XLA Modules:
  0.0 29.9 jit_solution(7410273751502388238)
XLA Ops:
  0.6 28.4 %shard_map.30 = (f32[8,64,256]{2,1,0:T(8,128)S(1)}, f32[1,128]{1,0:T(1,128)S(1)}) custom-call(f32[3,8,64,256]{3,2,1,0:T(8,128)} %u_hbm.1), custom_call_target="tpu_custom_call" | custom-call | tf_op jit(solution)/shard_map/pallas_call | solution.py:658
  29.0 0.0 copy-start
  29.0 0.9 %broadcast_multiply_fusion = f32[8,64,256]{2,1,0:T(8,128)} fusion(f32[8,64,256]{2,1,0:T(8,128)S(1)} %get-tuple-element.5, f32[64]{0:T(128)S(1)} %slice_bitcast_fusion), kind=kLoop, calls=%fused_computation | loop fusion | flops 131072 | bytes 1048832 | tf_op jit(solution)/shard_map/mul | solution.py:696
  29.9 0.0 copy-done
  (1 shorter events, 0.0 us)
Async XLA Ops:
  29.0 0.9 %copy-start = (f32[64]{0:T(128)}, f32[64]{0:T(128)S(1)}, u32[]{:S(2)}) copy-start(f32[64]{0:T(128)S(1)} %slice_bitcast_fusion) | copy-start | bytes 772

commit v3 on v2

--- a/solution.py
+++ b/solution.py
@@ -111,7 +111,16 @@
 
     barrier = pltpu.get_barrier_semaphore()
 
-    @pl.when(jnp.logical_not(closes))
+    even = lax.rem(gx, 2) == 0
+    paired = jnp.logical_or(jnp.logical_not(even), gx < n - 1)
+    waits_right = jnp.logical_and(jnp.logical_not(even), jnp.logical_not(closes))
+    later_left = jnp.logical_and(even, gx > 0)
+
+    @pl.when(paired)
+    def _():
+        signal(barrier, jnp.where(even, right, left), gy)
+
+    @pl.when(waits_right)
     def _():
         signal(barrier, right, gy)
 
@@ -123,14 +132,14 @@
     def _():
         signal(barrier, gx, gy + 1)
 
-    earlier = [jnp.where(x, 1, 0) for x in (gx > 0, closes, not_low)]
-    greeted = earlier[0] + earlier[1] + earlier[2]
+    earlier = [jnp.where(x, 1, 0) for x in (paired, later_left, closes, not_low)]
+    greeted = sum(earlier)
 
     @pl.when(greeted > 0)
     def _():
         pl.semaphore_wait(barrier, greeted)
 
-    @pl.when(gx > 0)
+    @pl.when(later_left)
     def _():
         signal(ready.at[0], left, gy)
 
@@ -282,7 +291,7 @@
             device_id_type=MESH,
         ).wait_send()
 
-    plans = (((0, 1, 2, 3), (), (), (), ()), ((), (), (0, 1, 2, 3), (), ()))
+    plans = (((0, 1), (2, 3), (), (), ()), ((0,), (), (1, 2, 3), (), ()))
     odd = lax.rem(gy, 2) == 1
 
     def start_all(point, sides=(0, 1)):
@@ -309,7 +318,7 @@
 
     own[1].wait()
 
-    @pl.when(closes)
+    @pl.when(jnp.logical_not(waits_right))
     def _():
         near_copy(1).start()
 
@@ -319,7 +328,7 @@
     def _():
         y_copy(0).start()
 
-    @pl.when(jnp.logical_not(closes))
+    @pl.when(waits_right)
     def _():
         pl.semaphore_wait(ready.at[0], 1)
         near_copy(1).start()

time: 30.1 us -> 29.5 us (0.980)
  Pallas kernels: 28.4 us -> 27.7 us
    pallas_call x1, Pallas kernels: 28.4 us -> 27.7 us  [local(): pl.pallas_call(functools.partial(kernel, n, m, nx, ny, shifts), out_shape...]
where the time goes in v3:
time: 29.5 us; the launch traced here: 29.3 us
  Pallas kernels  27.7 us (94%)
  other arithmetic  0.9 us (3%)
  between operations  0.65 us (2%)
    pallas_call x1, Pallas kernels, local(): pl.pallas_call(functools.partial(kernel, n, m, nx, ny, shifts), out_shape...  27.7 us
    mul x1, other arithmetic, local(): return (smooth, smooth[None, :, None] * strength)  0.9 us

profile of v3, /device:TPU:0, one launch (start us, length us, event | category | flops | bytes accessed | tf_op | source)
XLA Modules:
  0.0 29.3 jit_solution(2194648226970825040)
XLA Ops:
  0.6 27.7 %shard_map.30 = (f32[8,64,256]{2,1,0:T(8,128)S(1)}, f32[1,128]{1,0:T(1,128)S(1)}) custom-call(f32[3,8,64,256]{3,2,1,0:T(8,128)} %u_hbm.1), custom_call_target="tpu_custom_call" | custom-call | tf_op jit(solution)/shard_map/pallas_call | solution.py:667
  28.4 0.0 copy-start
  28.4 0.9 %broadcast_multiply_fusion = f32[8,64,256]{2,1,0:T(8,128)} fusion(f32[8,64,256]{2,1,0:T(8,128)S(1)} %get-tuple-element.5, f32[64]{0:T(128)S(1)} %slice_bitcast_fusion), kind=kLoop, calls=%fused_computation | loop fusion | flops 131072 | bytes 1048832 | tf_op jit(solution)/shard_map/mul | solution.py:705
  29.3 0.0 copy-done
  (1 shorter events, 0.0 us)
Async XLA Ops:
  28.4 0.9 %copy-start = (f32[64]{0:T(128)}, f32[64]{0:T(128)S(1)}, u32[]{:S(2)}) copy-start(f32[64]{0:T(128)S(1)} %slice_bitcast_fusion) | copy-start | bytes 772

commit v4 on v3

--- a/solution.py
+++ b/solution.py
@@ -72,6 +72,10 @@
     return edges
 
 
+def amounts_of(shifts):
+    return sorted({abs(s) for s in shifts} - {0})
+
+
 def kernel(n, m, nx, ny, shifts, u_hbm, strength, coef_ref, u, w, v, d, g, accn, accd,
            mine, mine_ends, gather, own_sem, xs_send, xs_recv, y_send, y_recv,
            c_recv, g_send, g_recv, ready, ring):
@@ -86,7 +90,7 @@
     shifting = any(shifts)
     cuts = cuts_of(nt)
     pieces = len(cuts) - 1
-    moved = cuts[max(pieces - 2, 1)]
+    amounts = amounts_of(shifts)
 
     def shift_at(index):
         value = jnp.int32(shifts[0])
@@ -203,8 +207,12 @@
     def near_copy(side):
         return x_copy(side, 1, 1, nt + 1, 0)
 
-    def moved_copy(side):
-        return x_copy(side, 3, moved, nt, pieces + 1)
+    def moved_tiles(j):
+        high = pieces - amounts[j - 1] if j else pieces
+        return cuts[pieces - amounts[j]], cuts[high]
+
+    def moved_copy(side, j):
+        return x_copy(side, 3, *moved_tiles(j), pieces + 1 + j)
 
     def far_parts(p):
         if p == 0:
@@ -216,16 +224,16 @@
             for low, high in far_parts(p):
                 x_copy(side, 2, low, high, p + 1).start()
 
-        if shifting and p >= pieces - 2:
-            pl.when(gains[side] <= 0)(run)
+        if shifting and p >= pieces - amounts[-1]:
+            pl.when(p < pieces - gains[side])(run)
         else:
             run()
 
     def start_moved(side):
-        if shifting:
-            @pl.when(gains[side] < 0)
+        for j in range(len(amounts)):
+            @pl.when(gains[side] <= -amounts[j])
             def _():
-                moved_copy(side).start()
+                moved_copy(side, j).start()
 
     def wait_far(side, p):
         count = cuts[p + 1] - cuts[p]
@@ -240,8 +248,10 @@
             if not shifting:
                 wait_rows(side, tiles_view(nt))
                 continue
-            for sign, count in ((0, nt), (1, moved), (-1, 2 * nt - moved)):
-                @pl.when(gains[side] == sign)
+            kept = [cuts[pieces - a] for a in amounts]
+            cases = [(0, nt)] + list(zip(amounts, kept)) + [(-a, 2 * nt - c) for a, c in zip(amounts, kept)]
+            for gain, count in cases:
+                @pl.when(gains[side] == gain)
                 def _():
                     wait_rows(side, tiles_view(count))
 
@@ -532,13 +542,13 @@
 
             return run
 
-        if not shifting or p < pieces - 2:
+        if not shifting or p < pieces - amounts[-1]:
             for side in range(2):
                 wait_far(side, p)
             lax.fori_loop(cuts[p], cuts[p + 1], both, 0)
             return
         for side in range(2):
-            @pl.when(gains[side] >= 0)
+            @pl.when(p < pieces + gains[side])
             def _():
                 wait_far(side, p)
                 lax.fori_loop(cuts[p], cuts[p + 1], one(side), 0)
@@ -592,16 +602,16 @@
         far(p)
         if p == 1:
             start_all(4)
-    if shifting:
-        for side in range(2):
-            def run(i, carry):
-                step(side, 3, i)
-                return carry
-
-            @pl.when(gains[side] > 0)
+    for side in range(2):
+        def run(i, carry):
+            step(side, 3, i)
+            return carry
+
+        for j in range(len(amounts)):
+            @pl.when(gains[side] >= amounts[j])
             def _():
-                moved_copy(1 - side).wait_recv()
-                lax.fori_loop(moved, nt, run, 0)
+                moved_copy(1 - side, j).wait_recv()
+                lax.fori_loop(*moved_tiles(j), run, 0)
 
     column_sums(mine)
 
@@ -688,7 +698,7 @@
             pltpu.VMEM((3, n, 2, lanes), f32),
             pltpu.SemaphoreType.DMA((3,)),
             pltpu.SemaphoreType.DMA((2,)),
-            pltpu.SemaphoreType.DMA((2, len(cuts_of(nt)) + (1 if any(shifts) else 0))),
+            pltpu.SemaphoreType.DMA((2, len(cuts_of(nt)) + len(amounts_of(shifts)))),
             pltpu.SemaphoreType.DMA((2,)),
             pltpu.SemaphoreType.DMA((2,)),
             pltpu.SemaphoreType.DMA((2,)),
@@ -707,7 +717,7 @@
 
 def solution(mesh):
     n, m = mesh.shape["gx"], mesh.shape["gy"]
-    shifts = (0,)*n
+    shifts = (0,) * (n - 2) + (1, 2)
     return jax.shard_map(
         functools.partial(local, n, m, shifts),
         mesh=mesh,

time: 29.5 us -> 29.2 us (0.990)
  Pallas kernels: 27.7 us -> 27.4 us
    pallas_call x1, Pallas kernels: 27.7 us -> 27.4 us  [local(): pl.pallas_call(functools.partial(kernel, n, m, nx, ny, shifts), out_shape...]
where the time goes in v4:
time: 29.2 us; the launch traced here: 29 us
  Pallas kernels  27.4 us (94%)
  other arithmetic  0.9 us (3%)
  between operations  0.65 us (2%)
    pallas_call x1, Pallas kernels, local(): pl.pallas_call(functools.partial(kernel, n, m, nx, ny, shifts), out_shape...  27.4 us
    mul x1, other arithmetic, local(): return (smooth, smooth[None, :, None] * strength)  0.9 us

profile of v4, /device:TPU:0, one launch (start us, length us, event | category | flops | bytes accessed | tf_op | source)
XLA Modules:
  0.0 29.0 jit_solution(15701585989309671807)
XLA Ops:
  0.6 27.4 %shard_map.30 = (f32[8,64,256]{2,1,0:T(8,128)S(1)}, f32[1,128]{1,0:T(1,128)S(1)}) custom-call(f32[3,8,64,256]{3,2,1,0:T(8,128)} %u_hbm.1), custom_call_target="tpu_custom_call" | custom-call | tf_op jit(solution)/shard_map/pallas_call | solution.py:677
  28.1 0.0 copy-start
  28.1 0.9 %broadcast_multiply_fusion = f32[8,64,256]{2,1,0:T(8,128)} fusion(f32[8,64,256]{2,1,0:T(8,128)S(1)} %get-tuple-element.5, f32[64]{0:T(128)S(1)} %slice_bitcast_fusion), kind=kLoop, calls=%fused_computation | loop fusion | flops 131072 | bytes 1048832 | tf_op jit(solution)/shard_map/mul | solution.py:715
  29.0 0.0 copy-done
  (1 shorter events, 0.0 us)
Async XLA Ops:
  28.1 0.9 %copy-start = (f32[64]{0:T(128)}, f32[64]{0:T(128)S(1)}, u32[]{:S(2)}) copy-start(f32[64]{0:T(128)S(1)} %slice_bitcast_fusion) | copy-start | bytes 772

commit v5 on v4

--- a/solution.py
+++ b/solution.py
@@ -301,7 +301,7 @@
             device_id_type=MESH,
         ).wait_send()
 
-    plans = (((0, 1), (2, 3), (), (), ()), ((0,), (), (1, 2, 3), (), ()))
+    plans = (((0, 1), (2, 3), (), (), ()), ((0,), (), (1, 2), (3,), ()))
     odd = lax.rem(gy, 2) == 1
 
     def start_all(point, sides=(0, 1)):

time: 29.2 us -> 28.9 us (0.990)
  no operation moved by 1% of the time
where the time goes in v5:
time: 28.9 us; the launch traced here: 28.7 us
  Pallas kernels  27.2 us (94%)
  other arithmetic  0.9 us (3%)
  between operations  0.65 us (2%)
    pallas_call x1, Pallas kernels, local(): pl.pallas_call(functools.partial(kernel, n, m, nx, ny, shifts), out_shape...  27.2 us
    mul x1, other arithmetic, local(): return (smooth, smooth[None, :, None] * strength)  0.9 us

profile of v5, /device:TPU:0, one launch (start us, length us, event | category | flops | bytes accessed | tf_op | source)
XLA Modules:
  0.0 28.7 jit_solution(8614153528102337088)
XLA Ops:
  0.6 27.2 %shard_map.30 = (f32[8,64,256]{2,1,0:T(8,128)S(1)}, f32[1,128]{1,0:T(1,128)S(1)}) custom-call(f32[3,8,64,256]{3,2,1,0:T(8,128)} %u_hbm.1), custom_call_target="tpu_custom_call" | custom-call | tf_op jit(solution)/shard_map/pallas_call | solution.py:677
  27.8 0.0 copy-start
  27.8 0.9 %broadcast_multiply_fusion = f32[8,64,256]{2,1,0:T(8,128)} fusion(f32[8,64,256]{2,1,0:T(8,128)S(1)} %get-tuple-element.5, f32[64]{0:T(128)S(1)} %slice_bitcast_fusion), kind=kLoop, calls=%fused_computation | loop fusion | flops 131072 | bytes 1048832 | tf_op jit(solution)/shard_map/mul | solution.py:715
  28.7 0.0 copy-done
  (1 shorter events, 0.0 us)
Async XLA Ops:
  27.8 0.9 %copy-start = (f32[64]{0:T(128)}, f32[64]{0:T(128)S(1)}, u32[]{:S(2)}) copy-start(f32[64]{0:T(128)S(1)} %slice_bitcast_fusion) | copy-start | bytes 772

commit v6 on v5

--- a/solution.py
+++ b/solution.py
@@ -301,7 +301,7 @@
             device_id_type=MESH,
         ).wait_send()
 
-    plans = (((0, 1), (2, 3), (), (), ()), ((0,), (), (1, 2), (3,), ()))
+    plans = (((0, 1, 2), (3,), (), (), ()), ((0,), (), (1, 2), (3,), ()))
     odd = lax.rem(gy, 2) == 1
 
     def start_all(point, sides=(0, 1)):

time: 28.9 us -> 28.9 us (level)
  Pallas kernels: 27.2 us -> 26.9 us
where the time goes in v6:
time: 28.9 us; the launch traced here: 28.5 us
  Pallas kernels  26.9 us (93%)
  other arithmetic  0.9 us (3%)
  between operations  0.65 us (2%)
    pallas_call x1, Pallas kernels, local(): pl.pallas_call(functools.partial(kernel, n, m, nx, ny, shifts), out_shape...  26.9 us
    mul x1, other arithmetic, local(): return (smooth, smooth[None, :, None] * strength)  0.9 us

profile of v6, /device:TPU:0, one launch (start us, length us, event | category | flops | bytes accessed | tf_op | source)
XLA Modules:
  0.0 28.5 jit_solution(10600441916336250417)
XLA Ops:
  0.6 26.9 %shard_map.30 = (f32[8,64,256]{2,1,0:T(8,128)S(1)}, f32[1,128]{1,0:T(1,128)S(1)}) custom-call(f32[3,8,64,256]{3,2,1,0:T(8,128)} %u_hbm.1), custom_call_target="tpu_custom_call" | custom-call | tf_op jit(solution)/shard_map/pallas_call | solution.py:677
  27.6 0.0 copy-start
  27.6 0.9 %broadcast_multiply_fusion = f32[8,64,256]{2,1,0:T(8,128)} fusion(f32[8,64,256]{2,1,0:T(8,128)S(1)} %get-tuple-element.5, f32[64]{0:T(128)S(1)} %slice_bitcast_fusion), kind=kLoop, calls=%fused_computation | loop fusion | flops 131072 | bytes 1048832 | tf_op jit(solution)/shard_map/mul | solution.py:715
  28.5 0.0 copy-done
  (1 shorter events, 0.0 us)
Async XLA Ops:
  27.6 0.9 %copy-start = (f32[64]{0:T(128)}, f32[64]{0:T(128)S(1)}, u32[]{:S(2)}) copy-start(f32[64]{0:T(128)S(1)} %slice_bitcast_fusion) | copy-start | bytes 772
